TPU v7x, 32 devices: a 4x4x1 block of a 4x4x8 slice. The times are simulated.
32 devices in a mesh: dp: 2 (over z, core), tp: 16 (over x, y).
Axes of the slice: x: 4, y: 4, z: 1, core: 2. Of those that a mesh axis runs over, the one named last changes fastest.
The devices are a block of a 4x4x8 slice.
Arguments:
- x: bfloat16 [4096, 8192], P('dp'), parts along dimension 0
- w_gate: bfloat16 [8192, 49152], P(None, 'tp')
- w_up: bfloat16 [8192, 49152], P(None, 'tp')
- w_down: bfloat16 [49152, 8192], P('tp')
Outputs:
- output: bfloat16 [4096, 8192], P('dp'), parts along dimension 0
There are 2 independent parts. A program takes and returns all parts, laid end to end along the dimension named above; an argument that names none is the same for every part.
All inputs are finite; a program needn't handle non-finite values.
Results may differ from a plain program's by a relative error of at most 0.016.
Values are sent between devices in bfloat16 or wider.
A program may use at most 768 MiB of HBM per device.

v0:
```python
import jax
import jax.numpy as jnp
from jax import lax
from jax.sharding import PartitionSpec as P


def solution(mesh):
    def step(x, w_gate, w_up, w_down):
        gate = jnp.dot(x, w_gate, preferred_element_type=jnp.float32)
        up = jnp.dot(x, w_up, preferred_element_type=jnp.float32)
        hidden = (jax.nn.silu(gate) * up).astype(jnp.bfloat16)
        term = jnp.dot(hidden, w_down, preferred_element_type=jnp.float32).astype(jnp.bfloat16)
        return lax.psum(term, "tp")

    return jax.shard_map(
        step,
        mesh=mesh,
        in_specs=(P("dp", None), P(None, "tp"), P(None, "tp"), P("tp", None)),
        out_specs=P("dp", None),
        check_vma=False,
    )
```

profile of v0, /device:TPU:97, one launch (start us, length us, event | category | flops | bytes accessed | tf_op | source)
XLA Modules:
  0.0 772.2 jit_solution(11491997347021330609)
XLA Ops:
  6.5 0.0 all-reduce.2.cloned.1.call-start
  6.6 116.1 %fusion = f32[2048,3072]{1,0:T(8,128)} fusion(bf16[2048,8192]{1,0:T(8,128)(2,1)} %param.4, bf16[8192,3072]{1,0:T(8,128)(2,1)} %param.5), kind=kOutput, calls=%fused_computation.2 | convolution fusion | flops 103079215104 | bytes 109051904 | tf_op jit(solution)/shard_map/dot_general | solution.py:9
  122.7 121.7 %multiply_convert_fusion = bf16[2048,3072]{1,0:T(8,128)(2,1)} fusion(f32[2048,3072]{1,0:T(8,128)} %fusion, bf16[2048,8192]{1,0:T(8,128)(2,1)} %param.4, bf16[8192,3072]{1,0:T(8,128)(2,1)} %param.6), kind=kOutput, calls=%fused_computation.1 | convolution fusion | flops 103116963840 | bytes 121634816 | tf_op jit(solution)/shard_map/dot_general | solution.py:10
  244.4 114.5 %convolution_convert_fusion = bf16[2048,8192]{1,0:T(8,128)(2,1)} fusion(bf16[2048,3072]{1,0:T(8,128)(2,1)} %multiply_convert_fusion, bf16[3072,8192]{1,0:T(8,128)(2,1)} %param.7), kind=kOutput, calls=%fused_computation | convolution fusion | flops 103095992320 | bytes 96468992 | tf_op jit(solution)/shard_map/dot_general | solution.py:12
  358.9 0.1 all-reduce.2.cloned.1.call-update
  358.9 383.4 %all-reduce.2.cloned.1.call-done = bf16[2048,8192]{1,0:T(8,128)(2,1)} async-done(((bf16[2048,8192]{1,0:T(8,128)(2,1)}), bf16[2048,8192]{1,0:T(8,128)(2,1)}) %all-reduce.2.cloned.1.call-update) | async-done | bytes 33554448 | tf_op jit(solution)/shard_map/psum | solution.py:13
  742.3 23.0 %copy.6 = bf16[2048,8192]{1,0:T(8,128)(2,1)} copy(bf16[2048,8192]{1,0:T(8,128)(2,1)} %all-reduce.2.cloned.1.call-done) | data formatting | bytes 67108864
Async XLA Ops:
  6.5 735.8 %all-reduce.2.cloned.1.call-start = ((), (), s32[]{:S(2)}) async-start(), calls=%async_computation | async-start | bytes 67108864 | tf_op jit(solution)/shard_map/psum | solution.py:13
Sparse Core Ops, SparseCore 0:
  359.1 383.2 all-reduce.1
where the time goes:
time: 772 us
  waiting for transfers between devices  383 us (50%)
  matrix products  352 us (46%)
  local copies, waits for them, and re-layouts  23 us (3%)
  between operations  13.4 us (2%)
    psum x1, waiting for transfers between devices, step(): return lax.psum(term, 'tp')  383 us
    dot_general x1, matrix products, step(): up = jnp.dot(x, w_up, preferred_element_type=jnp.float32)  122 us
    dot_general x1, matrix products, step(): gate = jnp.dot(x, w_gate, preferred_element_type=jnp.float32)  116 us
    dot_general x1, matrix products, step(): jnp.dot(hidden, w_down, preferred_element_type=jnp.float32)  115 us
    unnamed x1, local copies, waits for them, and re-layouts  23 us
  transfers between devices with their start and end apart: 1, of which 1 were waited for; matrix products, arithmetic and copies ran while one was open for 0% of the time, Pallas kernels for 0%

commit v1 on v0

v1 whole, which is shorter than its diff:
```python
import functools
import math

import jax
import jax.numpy as jnp
from jax import lax
from jax.experimental import pallas as pl
from jax.experimental.pallas import tpu as pltpu
from jax.sharding import PartitionSpec as P

MESH = pl.DeviceIdType.MESH
CHUNK = 512
GATE_TICKS = 12
STEPS = 6
STREAMS = ((0, 1), (0, -1), (1, 1), (1, -1))


def kernel(side, chunk, x_hbm, wg_hbm, wu_hbm, wd_hbm, y_hbm,
           x_v, h_v, wg_v, wu_v, wd_v, t_v, r1, s1, r2, s2,
           x_sem, wg_sem, wu_sem, wd_sem,
           r1_sem, s1_sem, r2_sem, s2_sem, g2_recv, g2_send, g1_recv, g1_send, own_sem,
           free1, free2):
    rows = x_hbm.shape[0]
    nk = rows // chunk
    rb = chunk // 2
    rs = rb // side
    tn = wg_v.shape[2]
    ct = wd_v.shape[2]
    gate_ticks = wg_hbm.shape[1] // tn
    down_ticks = 4 * side
    ticks = gate_ticks + down_ticks
    me = lax.axis_index("tp")
    pos = (me // side, me % side)

    def device(axis, shift):
        p0, p1 = pos
        if axis == 0:
            p0 = (p0 + shift + side) % side
        else:
            p1 = (p1 + shift + side) % side
        return {"tp": p0 * side + p1}

    barrier = pltpu.get_barrier_semaphore()
    for axis, shift in STREAMS:
        pl.semaphore_signal(barrier, inc=1, device_id=device(axis, shift), device_id_type=MESH)
    pl.semaphore_wait(barrier, 4)

    def x_copy(k):
        return pltpu.make_async_copy(x_hbm.at[pl.ds(k * chunk, chunk), :], x_v, x_sem)

    def gate_copies(j):
        cols = pl.ds(pl.multiple_of(j * tn, tn), tn)
        s = j % 2
        return (
            pltpu.make_async_copy(wg_hbm.at[:, cols], wg_v.at[s], wg_sem.at[s]),
            pltpu.make_async_copy(wu_hbm.at[:, cols], wu_v.at[s], wu_sem.at[s]),
        )

    def down_copy(q):
        c, step = q % 4, q // 4
        along = jnp.where(c < 2, pos[0], pos[1])
        way = 1 - 2 * (c % 2)
        piece = (along - way * (1 + step) + 2 * side) % side
        cols = pl.ds(pl.multiple_of((c * side + piece) * ct, ct), ct)
        s = q % 2
        return pltpu.make_async_copy(wd_hbm.at[:, cols], wd_v.at[s], wd_sem.at[s])

    def piece1(c, e):
        axis, way = STREAMS[c]
        return (pos[axis] - way * (1 + e) + 3 * side) % side

    def piece2(c, e):
        axis, way = STREAMS[c]
        return (pos[1 - axis] - way * (1 + e) + 3 * side) % side

    def to1(c):
        axis, way = STREAMS[c]
        return device(axis, way)

    def from1(c):
        axis, way = STREAMS[c]
        return device(axis, -way)

    def to2(c):
        axis, way = STREAMS[c]
        return device(1 - axis, way)

    def from2(c):
        axis, way = STREAMS[c]
        return device(1 - axis, -way)

    def rs1_copy(k, b, c, hop):
        slot = ((side - 1) * k + hop) % 2
        return pltpu.make_async_remote_copy(
            src_ref=s1.at[b, c], dst_ref=r1.at[b, c, slot],
            send_sem=s1_sem.at[b, c], recv_sem=r1_sem.at[b, c, slot],
            device_id=to1(c), device_id_type=MESH), slot

    def rs2_copy(k, b, c, hop):
        slot = ((side - 1) * k + hop) % 2
        return pltpu.make_async_remote_copy(
            src_ref=s2.at[b, c], dst_ref=r2.at[b, c, slot],
            send_sem=s2_sem.at[b, c], recv_sem=r2_sem.at[b, c, slot],
            device_id=to2(c), device_id_type=MESH), slot

    def y_at(k, b, c, row, nrows, piece):
        return y_hbm.at[
            pl.ds(pl.multiple_of(k * chunk + b * rb + row, rs), nrows),
            pl.ds(pl.multiple_of((c * side + piece) * ct, ct), ct)]

    def ag2_copy(k, b, c, hop):
        ref = y_at(k, b, c, piece2(c, hop - 1) * rs, rs, piece1(c, -1))
        return pltpu.make_async_remote_copy(
            src_ref=s2.at[b, c] if hop == 0 else ref, dst_ref=ref,
            send_sem=g2_send.at[b, c], recv_sem=g2_recv.at[b, c, hop, k % 2],
            device_id=to2(c), device_id_type=MESH)

    def ag2_arrival(k, b, c, hop):
        ref = y_at(k, b, c, piece2(c, hop) * rs, rs, piece1(c, -1))
        return pltpu.make_async_remote_copy(
            src_ref=ref, dst_ref=ref,
            send_sem=g2_send.at[b, c], recv_sem=g2_recv.at[b, c, hop, k % 2],
            device_id=to2(c), device_id_type=MESH)

    def ag1_copy(k, b, c, hop):
        ref = y_at(k, b, c, 0, rb, piece1(c, hop - 1))
        return pltpu.make_async_remote_copy(
            src_ref=ref, dst_ref=ref,
            send_sem=g1_send.at[b, c], recv_sem=g1_recv.at[b, c, hop, k % 2],
            device_id=to1(c), device_id_type=MESH)

    def ag1_arrival(k, b, c, hop):
        ref = y_at(k, b, c, 0, rb, piece1(c, hop))
        return pltpu.make_async_remote_copy(
            src_ref=ref, dst_ref=ref,
            send_sem=g1_send.at[b, c], recv_sem=g1_recv.at[b, c, hop, k % 2],
            device_id=to1(c), device_id_type=MESH)

    def own_copy(k, b, c):
        return pltpu.make_async_copy(
            s2.at[b, c], y_at(k, b, c, piece2(c, -1) * rs, rs, piece1(c, -1)), own_sem.at[b, c])

    last = side - 1

    def event(e, k, b):
        half = pl.ds(pl.multiple_of(b * rb, rb), rb)
        for c in range(4):
            if e < last:
                copy, _ = rs1_copy(k, b, c, e)
                if e == 0:
                    s1[b, c] = t_v[c, e, half, :].astype(jnp.bfloat16)
                else:
                    prev, slot = rs1_copy(k, b, c, e - 1)
                    prev.wait_recv()
                    prev.wait_send()
                    s1[b, c] = (r1[b, c, slot].astype(jnp.float32) + t_v[c, e, half, :]).astype(jnp.bfloat16)

                    @pl.when((side - 1) * k + (e - 1) < (side - 1) * nk - 2)
                    def _():
                        pl.semaphore_signal(free1.at[b, c], inc=1, device_id=from1(c), device_id_type=MESH)

                @pl.when((side - 1) * k + e >= 2)
                def _():
                    pl.semaphore_wait(free1.at[b, c], 1)

                copy.start()
            elif e < 2 * last:
                f = e - last
                if f == 0:
                    prev, slot = rs1_copy(k, b, c, last - 1)
                    prev.wait_recv()
                    prev.wait_send()
                    t_v[c, last, half, :] = r1[b, c, slot].astype(jnp.float32) + t_v[c, last, half, :]

                    @pl.when((side - 1) * k + (last - 1) < (side - 1) * nk - 2)
                    def _():
                        pl.semaphore_signal(free1.at[b, c], inc=1, device_id=from1(c), device_id_type=MESH)

                part = pl.ds(pl.multiple_of(b * rb + piece2(c, f) * rs, rs), rs)
                if f == 0:
                    s2[b, c] = t_v[c, last, part, :].astype(jnp.bfloat16)
                else:
                    prev, slot = rs2_copy(k, b, c, f - 1)
                    prev.wait_recv()
                    prev.wait_send()
                    s2[b, c] = (r2[b, c, slot].astype(jnp.float32) + t_v[c, last, part, :]).astype(jnp.bfloat16)

                    @pl.when((side - 1) * k + (f - 1) < (side - 1) * nk - 2)
                    def _():
                        pl.semaphore_signal(free2.at[b, c], inc=1, device_id=from2(c), device_id_type=MESH)

                @pl.when((side - 1) * k + f >= 2)
                def _():
                    pl.semaphore_wait(free2.at[b, c], 1)

                copy, _ = rs2_copy(k, b, c, f)
                copy.start()
            elif e < 3 * last:
                f = e - 2 * last
                if f == 0:
                    part = pl.ds(pl.multiple_of(b * rb + piece2(c, last) * rs, rs), rs)
                    prev, slot = rs2_copy(k, b, c, last - 1)
                    prev.wait_recv()
                    prev.wait_send()
                    s2[b, c] = (r2[b, c, slot].astype(jnp.float32) + t_v[c, last, part, :]).astype(jnp.bfloat16)

                    @pl.when((side - 1) * k + (last - 1) < (side - 1) * nk - 2)
                    def _():
                        pl.semaphore_signal(free2.at[b, c], inc=1, device_id=from2(c), device_id_type=MESH)

                    own_copy(k, b, c).start()
                else:
                    ag2_arrival(k, b, c, f - 1).wait_recv()
                    ag2_copy(k, b, c, f - 1).wait_send()
                    if f == 1:
                        own_copy(k, b, c).wait()
                ag2_copy(k, b, c, f).start()
            elif e < 4 * last:
                f = e - 3 * last
                if f == 0:
                    ag2_arrival(k, b, c, last - 1).wait_recv()
                    ag2_copy(k, b, c, last - 1).wait_send()
                else:
                    ag1_arrival(k, b, c, f - 1).wait_recv()
                    ag1_copy(k, b, c, f - 1).wait_send()
                ag1_copy(k, b, c, f).start()
            else:
                ag1_arrival(k, b, c, last - 1).wait_recv()
                ag1_copy(k, b, c, last - 1).wait_send()

    def communicate(g):
        b = g % 2
        u = g // 2
        k1 = u // STEPS
        e1 = u % STEPS

        @pl.when((e1 == 0) & (k1 >= 2))
        def _():
            event(2 * STEPS, k1 - 2, b)

        for e in range(STEPS):
            @pl.when((e1 == e) & (k1 >= 1) & (k1 <= nk))
            def _():
                event(e + STEPS, k1 - 1, b)

            @pl.when((e1 == e) & (k1 < nk))
            def _():
                event(e, k1, b)

    x_copy(0).start()
    for copy in gate_copies(0):
        copy.start()

    @pl.loop(0, (nk + 2) * ticks)
    def _(n):
        k = n // ticks
        t = n % ticks
        q = t - gate_ticks

        @pl.when((k < nk) & (t < gate_ticks))
        def _():
            @pl.when(t == 0)
            def _():
                x_copy(k).wait()

            for copy in gate_copies(t):
                copy.wait()

            @pl.when(t + 1 < gate_ticks)
            def _():
                for copy in gate_copies(t + 1):
                    copy.start()

            @pl.when(t == gate_ticks - 2)
            def _():
                down_copy(0).start()

            s = t % 2
            for i in range(2):
                part = slice(i * chunk // 2, (i + 1) * chunk // 2)
                gate = jnp.dot(x_v[part, :], wg_v[s], preferred_element_type=jnp.float32)
                up = jnp.dot(x_v[part, :], wu_v[s], preferred_element_type=jnp.float32)
                h_v[part, pl.ds(pl.multiple_of(t * tn, tn), tn)] = (gate * jax.nn.sigmoid(gate) * up).astype(jnp.bfloat16)

        @pl.when((k < nk) & (t >= gate_ticks))
        def _():
            down_copy(q).wait()

            @pl.when(q + 1 < down_ticks)
            def _():
                down_copy(q + 1).start()

            @pl.when((q == 0) & (k + 1 < nk))
            def _():
                x_copy(k + 1).start()

            @pl.when((q == down_ticks // 2) & (k + 1 < nk))
            def _():
                for copy in gate_copies(0):
                    copy.start()

            for i in range(2):
                part = slice(i * chunk // 2, (i + 1) * chunk // 2)
                t_v[q % 4, q // 4, part, :] = jnp.dot(h_v[part, :], wd_v[q % 2], preferred_element_type=jnp.float32)

        @pl.when((k > 0) & (t < gate_ticks) & (t % 3 > 0))
        def _():
            communicate(2 * STEPS * (k - 1) + 4 + (t // 3) * 2 + t % 3 - 1)

        @pl.when((t >= gate_ticks) & (q % 4 == 3) & (2 * STEPS * k + q // 4 < 2 * STEPS * (nk + 1) + 2))
        def _():
            communicate(2 * STEPS * k + q // 4)


def solution(mesh):
    side = math.isqrt(mesh.shape["tp"])

    def step(x, w_gate, w_up, w_down):
        rows, d = x.shape
        f = w_gate.shape[1]
        chunk = min(CHUNK, rows)
        tn, ct, rb = f // GATE_TICKS, d // (4 * side), chunk // 2
        rs = rb // side
        bf16, f32 = jnp.bfloat16, jnp.float32
        dma = pltpu.SemaphoreType.DMA
        return pl.pallas_call(
            functools.partial(kernel, side, chunk),
            out_shape=jax.ShapeDtypeStruct((rows, d), bf16),
            in_specs=[pl.BlockSpec(memory_space=pl.ANY)] * 4,
            out_specs=pl.BlockSpec(memory_space=pl.ANY),
            scratch_shapes=[
                pltpu.VMEM((chunk, d), bf16),
                pltpu.VMEM((chunk, f), bf16),
                pltpu.VMEM((2, d, tn), bf16),
                pltpu.VMEM((2, d, tn), bf16),
                pltpu.VMEM((2, f, ct), bf16),
                pltpu.VMEM((4, side, chunk, ct), f32),
                pltpu.VMEM((2, 4, 2, rb, ct), bf16),
                pltpu.VMEM((2, 4, rb, ct), bf16),
                pltpu.VMEM((2, 4, 2, rs, ct), bf16),
                pltpu.VMEM((2, 4, rs, ct), bf16),
                dma, dma((2,)), dma((2,)), dma((2,)),
                dma((2, 4, 2)), dma((2, 4)), dma((2, 4, 2)), dma((2, 4)),
                dma((2, 4, side - 1, 2)), dma((2, 4)), dma((2, 4, side - 1, 2)), dma((2, 4)), dma((2, 4)),
                pltpu.SemaphoreType.REGULAR((2, 4)), pltpu.SemaphoreType.REGULAR((2, 4)),
            ],
            compiler_params=pltpu.CompilerParams(
                collective_id=0, has_side_effects=True, vmem_limit_bytes=67043328),
        )(x, w_gate, w_up, w_down)

    return jax.shard_map(
        step,
        mesh=mesh,
        in_specs=(P("dp", None), P(None, "tp"), P(None, "tp"), P("tp", None)),
        out_specs=P("dp", None),
        check_vma=False,
    )
```

time: 772 us -> 521 us (0.67)
  Pallas kernels: 0 us -> 496 us
  waiting for transfers between devices: 383 us -> 0 us
  matrix products: 352 us -> 0 us
  between operations: 13.4 us -> 0.01 us
    pallas_call x0 -> x1, Pallas kernels: none -> 496 us  [step(): pl.pallas_call(functools.partial(kernel, side, chunk), out_shape=jax.Shap...]
    psum x1 -> x0, waiting for transfers between devices: 383 us -> none  [step(): return lax.psum(term, 'tp')]
    dot_general x3 -> x0, matrix products: 352 us -> none  [the longest x1 122 us: step(): up = jnp.dot(x, w_up, preferred_element_type=jnp.float32)]
  transfers between devices with their start and end apart: 1 -> 0, of which waited for: 1 -> 0; matrix products, arithmetic and copies ran while one was open for 0% -> 0% of each run, Pallas kernels for 0% -> 0%
where the time goes in v1:
time: 521 us; the launch traced here: 519 us
  Pallas kernels  496 us (95%)
  local copies, waits for them, and re-layouts  23 us (4%)
    pallas_call x1, Pallas kernels, step(): pl.pallas_call(functools.partial(kernel, side, chunk), out_shape=jax.Shap...  496 us
    unnamed x1, local copies, waits for them, and re-layouts  23 us

profile of v1, /device:TPU:97, one launch (start us, length us, event | category | flops | bytes accessed | tf_op | source)
XLA Modules:
  0.0 519.2 jit_solution(17403678630121249329)
XLA Ops:
  0.0 496.2 %shard_map.46 = bf16[2048,8192]{1,0:T(8,128)(2,1)} custom-call(bf16[2048,8192]{1,0:T(8,128)(2,1)} %x_hbm.1, bf16[8192,3072]{1,0:T(8,128)(2,1)} %wg_hbm.1, bf16[8192,3072]{1,0:T(8,128)(2,1)} %wu_hbm.1, bf16[3072,8192]{1,0:T(8,128)(2,1)} %wd_hbm.1), custom_call_target="tpu_custom_call" | custom-call | tf_op jit(solution)/shard_map/pallas_call | solution.py:326
  496.2 23.0 %copy.6 = bf16[2048,8192]{1,0:T(8,128)(2,1)} copy(bf16[2048,8192]{1,0:T(8,128)(2,1)} %shard_map.46) | data formatting | bytes 67108864
